TPU v7x, 32 devices: a whole 2x2x4 slice. The times are simulated.
32 devices in a mesh: row: 8 (over z, core), col: 4 (over y, x).
Axes of the slice: x: 2, y: 2, z: 4, core: 2. Of those that a mesh axis runs over, the one named last changes fastest.
Arguments:
- reference_image: float32 [1024, 1024], P('row', 'col'), may hold values from -6 to 6
- source_images: float32 [4, 1024, 1024], P(None, 'row', 'col'), may hold values from -6 to 6
- hypotheses: int32 [8, 1024, 1024], P(None, 'row', 'col'), may hold values from 0 to 15
- source_ids: int32 [4], replicated, may hold values from 1 to 3
- coarse_disp: float32 [128, 128], P('col'), may hold values from 0 to 15
- coarse_conf: float32 [128, 128], P('col'), may hold values from 0.1 to 10
Outputs:
- disparity: float32 [1024, 1024], P('row', 'col')
All inputs are finite; a program needn't handle non-finite values.
Results may differ from a plain program's by a relative error of at most 0.0003.
Values sent between devices are 32-bit elements; how exact they have to be, the bound alone decides.
A program may use at most 64 MiB of HBM per device.

v0:
```python
import jax
import jax.numpy as jnp
from jax import lax
from jax.sharding import PartitionSpec as P

LEVELS = 16
HYP = 8
SRC = 4
WIN = 11
UPS = 8
CITER = 4
HALO = 50


smooth_pull = 1.0
previous_estimate_factor = 0.01
exponential_sharpness = 0.1
variance_floor = 1e-05


def extended_2(array, sides, width):
    for axis, dim in sides:
        size, length = (lax.axis_size(axis), array.shape[dim])
        up = [(i, (i + 1) % size) for i in range(size - 1)]
        down = [(j, i) for i, j in up]
        last = lax.slice_in_dim(array, length - width, length, axis=dim)
        initial = lax.slice_in_dim(array, 0, width, axis=dim)
        before = lax.ppermute(last, axis, up)
        after = lax.ppermute(initial, axis, down)
        array = jnp.concatenate([before, array, after], axis=dim)
    return array


def interp_matrix(fine_start, fine_count, coarse_start, coarse_pixel_number, coarse_total):
    fine_pos = fine_start + jnp.arange(fine_count, dtype=jnp.int32)
    numerator = 2 * fine_pos + 1 - UPS
    lower = numerator // (2 * UPS)
    fraction = (numerator - lower * 2 * UPS).astype(jnp.float32) / (2.0 * UPS)
    low_index = jnp.clip(lower, 0, coarse_total - 1) - coarse_start
    high_index = jnp.clip(lower + 1, 0, coarse_total - 1) - coarse_start
    columns = jnp.arange(coarse_pixel_number, dtype=jnp.int32)
    low_part = jnp.where(columns[None, :] == low_index[:, None], 1.0 - fraction[:, None], 0.0)
    high_part = jnp.where(columns[None, :] == high_index[:, None], fraction[:, None], 0.0)
    return low_part + high_part


def jacobi_step(padded_line_span, disp, conf):
    middle = padded_line_span[1:-1]
    col_pad = jnp.pad(middle, ((0, 0), (1, 1)))
    neighbours = padded_line_span[:-2] + padded_line_span[2:] + col_pad[:, :-2] + col_pad[:, 2:]
    return (conf * disp + smooth_pull * neighbours) / (conf + 4.0 * smooth_pull)


def band_matrix(count):
    rows_pos = jnp.arange(count, dtype=jnp.int32)[:, None]
    cols_pos = jnp.arange(count + WIN - 1, dtype=jnp.int32)[None, :]
    offsets = cols_pos - rows_pos
    return jnp.where((offsets >= 0) & (offsets < WIN), 1.0, 0.0).astype(jnp.float32)


def window_box(maps, row_band, col_band):
    summed = jnp.einsum("ij,mjk->mik", row_band, maps, precision=lax.Precision.HIGHEST)
    return jnp.einsum("mik,lk->mil", summed, col_band, precision=lax.Precision.HIGHEST)


def estimate(chosen_hypothesis, candidate, centre):
    neighbour_jump_cost = (
        1.0 - chosen_hypothesis + previous_estimate_factor * (candidate - centre[None]) ** 2
    )
    candidate_mixing_shares = jnp.exp(-neighbour_jump_cost / exponential_sharpness)
    return jnp.sum(candidate_mixing_shares * candidate, axis=0) / jnp.sum(
        candidate_mixing_shares, axis=0
    )


def on_device(reference_image, source_images, hypotheses, source_ids, coarse_disp, coarse_conf):
    rows_tile, cols_tile = reference_image.shape
    row_count = lax.axis_size("row")
    col_count = lax.axis_size("col")
    row_index = lax.axis_index("row")
    col_index = lax.axis_index("col")
    radius = WIN // 2
    coarse_tile = rows_tile // UPS
    block_rows, coarse_cols = coarse_disp.shape
    coarse_height = block_rows * col_count
    whole_disp, whole_image_confidence = (
        lax.all_gather(coarse_disp, "col", axis=0, tiled=True),
        lax.all_gather(coarse_conf, "col", axis=0, tiled=True),
    )
    current = whole_disp
    for sweep in range(CITER):
        current = jacobi_step(
            jnp.pad(current, ((1, 1), (0, 0))), whole_disp, whole_image_confidence
        )
    padded_all = jnp.pad(current, ((1, 1), (0, 0)))
    coarse_piece = lax.dynamic_slice_in_dim(padded_all, row_index * coarse_tile, coarse_tile + 2, 0)
    row_mat = interp_matrix(
        row_index * rows_tile,
        rows_tile,
        row_index * coarse_tile - 1,
        coarse_tile + 2,
        coarse_height,
    )
    column_interp_weights = interp_matrix(
        col_index * cols_tile, cols_tile, 0, coarse_cols, coarse_cols
    )
    upsampled = jnp.dot(
        jnp.dot(row_mat, coarse_piece, precision=lax.Precision.HIGHEST),
        column_interp_weights.T,
        precision=lax.Precision.HIGHEST,
    )
    stacked = jnp.concatenate([reference_image[None], source_images], 0)
    padded_all = extended_2(stacked, (("row", 1), ("col", 2)), HALO)
    extended = padded_all[:, HALO - radius : HALO + rows_tile + radius, : HALO + cols_tile + radius]
    area = float(WIN * WIN)
    extended_width = extended.shape[2]
    row_band = band_matrix(rows_tile)
    wide_band = band_matrix(extended_width - 2 * radius)
    narrow_band = band_matrix(cols_tile)
    moments = (
        window_box(jnp.concatenate([extended, extended * extended], 0), row_band, wide_band) / area
    )
    channels = SRC + 1
    wide_mean = moments[:channels]
    wide_var = moments[channels:] - wide_mean**2 + variance_floor
    ref_begin = HALO - radius
    ref_mean = wide_mean[0][:, ref_begin : ref_begin + cols_tile]
    ref_var = wide_var[0][:, ref_begin : ref_begin + cols_tile]
    ref_window = extended[0][:, ref_begin : ref_begin + cols_tile + 2 * radius]

    def level_step(depth_level, chosen_hypothesis):
        begins = []
        elementwise_multiples = []
        for view_slot in range(SRC):
            begin_col = ref_begin - source_ids[view_slot] * depth_level
            begins.append(begin_col)
            src_window = lax.dynamic_slice_in_dim(
                extended[view_slot + 1], begin_col, cols_tile + 2 * radius, 1
            )
            elementwise_multiples.append(ref_window * src_window)
        cross_sums = window_box(jnp.stack(elementwise_multiples), row_band, narrow_band) / area
        ncc_sum = jnp.zeros((rows_tile, cols_tile), jnp.float32)
        for view_slot in range(SRC):
            mean_src = lax.dynamic_slice_in_dim(
                wide_mean[view_slot + 1], begins[view_slot], cols_tile, 1
            )
            var_src = lax.dynamic_slice_in_dim(
                wide_var[view_slot + 1], begins[view_slot], cols_tile, 1
            )
            ncc_sum = ncc_sum + (cross_sums[view_slot] - ref_mean * mean_src) / jnp.sqrt(
                ref_var * var_src
            )
        volume = ncc_sum / SRC
        return chosen_hypothesis + jnp.where(hypotheses == depth_level, volume[None], 0.0)

    chosen_hypothesis = lax.fori_loop(
        0, LEVELS, level_step, jnp.zeros((HYP, rows_tile, cols_tile), jnp.float32)
    )
    candidate = hypotheses.astype(jnp.float32)
    red = estimate(chosen_hypothesis, candidate, upsampled)
    red_ext = extended_2(red, (("row", 0), ("col", 1)), 1)
    neighbours = red_ext[:-2, 1:-1] + red_ext[2:, 1:-1] + red_ext[1:-1, :-2] + red_ext[1:-1, 2:]
    row_pos = row_index * rows_tile + jnp.arange(rows_tile, dtype=jnp.int32)
    col_pos = col_index * cols_tile + jnp.arange(cols_tile, dtype=jnp.int32)
    image_rows = rows_tile * row_count
    image_column_count = cols_tile * col_count
    vertical_strip_bounds = (row_pos == 0).astype(jnp.float32) + (row_pos == image_rows - 1).astype(
        jnp.float32
    )
    col_edges = (col_pos == 0).astype(jnp.float32) + (col_pos == image_column_count - 1).astype(
        jnp.float32
    )
    counted = 4.0 - vertical_strip_bounds[:, None] - col_edges[None, :]
    centre = 0.5 * upsampled + 0.5 * neighbours / counted
    black = estimate(chosen_hypothesis, candidate, centre)
    parity = (row_pos[:, None] + col_pos[None, :]) % 2 == 0
    return jnp.where(parity, red, black)


def solution(mesh):
    in_specs = (
        P("row", "col"),
        P(None, "row", "col"),
        P(None, "row", "col"),
        P(),
        P("col", None),
        P("col", None),
    )
    out_specs = P("row", "col")
    return jax.shard_map(
        on_device, mesh=mesh, in_specs=in_specs, out_specs=out_specs, check_vma=False
    )
```

profile of v0, /device:TPU:0, one launch (start us, length us, event | category | flops | bytes accessed | tf_op | source)
XLA Modules:
  0.0 290.2 jit_solution(7487293340198000590)
XLA Ops:
  2.5 3.1 %collective-permute-start = (f32[5,50,256]{2,1,0:T(8,128)S(1)}, f32[5,50,256]{2,1,0:T(8,128)S(1)}, u32[]{:S(2)}, u32[]{:S(2)}) collective-permute-start(f32[5,50,256]{2,1,0:T(8,128)S(1)} %get-tuple-element.455), channel_id=1, source_target_pairs={{0,4},{4,8},{8,12},{12,16},{16,20},{20,24},{24,28},{1,5},{5,9},{9,... | collective-permute-start | bytes 768008 | tf_op jit(solution)/shard_map/ppermute | solution.py:28
  5.7 9.7 %all_gather.7 = f32[128,128]{1,0:T(8,128)S(1)} all-gather(f32[32,128]{1,0:T(8,128)S(1)} %copy-done.13), channel_id=1, replica_groups=mesh['row'=8,'col'=4] {'col'}, dimensions={0}, use_global_device_ids=true | all-gather | bytes 81920 | tf_op jit(solution)/shard_map/all_gather | solution.py:87
  15.4 8.2 %all_gather.6 = f32[128,128]{1,0:T(8,128)S(1)} all-gather(f32[32,128]{1,0:T(8,128)S(1)} %copy-done.14), channel_id=1, replica_groups=mesh['row'=8,'col'=4] {'col'}, dimensions={0}, use_global_device_ids=true | all-gather | bytes 81920 | tf_op jit(solution)/shard_map/all_gather | solution.py:88
  27.3 4.7 %collective-permute-start.2 = (f32[5,228,50]{1,2,0:T(8,128)S(1)}, f32[5,228,50]{1,2,0:T(8,128)S(1)}, u32[]{:S(2)}, u32[]{:S(2)}) collective-permute-start(f32[5,228,50]{1,2,0:T(8,128)S(1)} %copy.19), channel_id=1, source_target_pairs={{0,1},{1,2},{2,3},{4,5},{5,6},{6,7},{8,9},{9,10},{10,11},{12,13},{... | collective-permute-start | bytes 684008 | tf_op jit(solution)/shard_map/ppermute | solution.py:28
  33.1 3.9 %collective-permute-done.3 = f32[5,228,50]{1,2,0:T(8,128)S(1)} collective-permute-done((f32[5,228,50]{1,2,0:T(8,128)}, f32[5,228,50]{1,2,0:T(8,128)S(1)}, u32[]{:S(2)}, u32[]{:S(2)}) %collective-permute-start.3) | collective-permute-done | bytes 228032 | tf_op jit(solution)/shard_map/ppermute | solution.py:29
  39.1 1.6 fusion.150
  40.8 5.9 %fusion.55 = f32[10,311,128]{2,1,0:T(8,128)S(1)} fusion(f32[5,138,311]{2,1,0:T(8,128)S(1)} %get-tuple-element.425, f32[5,138,311]{2,1,0:T(8,128)S(1)} %get-tuple-element.574), kind=kOutput, calls=%fused_computation.70 | convolution fusion | flops 659737984 | bytes 3309040 | tf_op jit(solution)/shard_map/ij,mjk->mik/dot_general | solution.py:62
  46.7 2.7 fusion.61
  52.6 2.4 copy.26
  57.7 2.5 copy.24
  61.0 212.8 %while.17 = (s32[]{:T(128)}, f32[8,128,256]{2,1,0:T(8,128)S(1)}, s32[8,128,256]{2,1,0:T(8,128)S(1)}, f32[138,266]{1,0:T(8,128)}, f32[5,138,311]{2,1,0:T(8,128)S(...) while((s32[]{:T(128)}, f32[8,128,256]{2,1,0:T(8,128)S(1)}, ...), condition=%wide.region_1.2_spmd.clone, body=%wide.region_0.1_spmd.clone.sunk | while | flops 646766912 | bytes 25636720 | solution.py:156
  66.8 2.3 convolution_bitcast_fusion.2
  71.4 1.6 fusion.175
  80.0 2.3 convolution_bitcast_fusion.2
  84.7 1.6 fusion.175
  93.3 2.3 convolution_bitcast_fusion.2
  98.0 1.6 fusion.175
  106.6 2.3 convolution_bitcast_fusion.2
  111.3 1.6 fusion.175
  119.9 2.3 convolution_bitcast_fusion.2
  124.6 1.6 fusion.175
  133.2 2.3 convolution_bitcast_fusion.2
  137.9 1.6 fusion.175
  144.9 1.6 bitcast_multiply_fusion.13
  146.5 2.3 convolution_bitcast_fusion.2
  151.2 1.6 fusion.175
  158.2 1.6 bitcast_multiply_fusion.13
  159.8 2.3 convolution_bitcast_fusion.2
  164.5 1.6 fusion.175
  173.1 2.3 convolution_bitcast_fusion.2
  177.8 1.6 fusion.175
  186.4 2.3 convolution_bitcast_fusion.2
  191.1 1.6 fusion.175
  199.7 2.3 convolution_bitcast_fusion.2
  204.4 1.6 fusion.175
  213.0 2.3 convolution_bitcast_fusion.2
  217.7 1.6 fusion.175
  226.3 2.3 convolution_bitcast_fusion.2
  231.0 1.6 fusion.175
  239.6 2.3 convolution_bitcast_fusion.2
  244.3 1.6 fusion.175
  252.9 2.3 convolution_bitcast_fusion.2
  257.6 1.6 fusion.175
  266.2 2.3 convolution_bitcast_fusion.2
  270.8 1.6 fusion.175
  276.5 3.0 %collective-permute-start.4 = (f32[1,256]{1,0:T(1,128)S(1)}, f32[1,256]{1,0:T(1,128)S(1)}, u32[]{:S(2)}, u32[]{:S(2)}) collective-permute-start(f32[1,256]{1,0:T(1,128)S(1)} %get-tuple-element.459), channel_id=1, source_target_pairs={{0,4},{4,8},{8,12},{12,16},{16,20},{20,24},{24,28},{1,5},{5,9},{9,... | collective-permute-start | bytes 3080 | tf_op jit(solution)/shard_map/ppermute | solution.py:28
  281.8 4.5 %collective-permute-start.6 = (f32[130,1]{1,0:T(8,128)S(1)}, f32[130,1]{1,0:T(8,128)S(1)}, u32[]{:S(2)}, u32[]{:S(2)}) collective-permute-start(f32[130,1]{1,0:T(8,128)S(1)} %get-tuple-element.457), channel_id=1, source_target_pairs={{0,1},{1,2},{2,3},{4,5},{5,6},{6,7},{8,9},{9,10},{10,11},{12,13},{... | collective-permute-start | bytes 1568 | tf_op jit(solution)/shard_map/ppermute | solution.py:28
  287.1 1.7 collective-permute-done.6
  (293 shorter events, 127.5 us)
Async XLA Ops:
  0.0 5.7 %copy-start.13 = (f32[32,128]{1,0:T(8,128)S(1)}, f32[32,128]{1,0:T(8,128)}, u32[]{:S(2)}) copy-start(f32[32,128]{1,0:T(8,128)} %param.12) | copy-start | bytes 49156
  0.0 15.4 %copy-start.14 = (f32[32,128]{1,0:T(8,128)S(1)}, f32[32,128]{1,0:T(8,128)}, u32[]{:S(2)}) copy-start(f32[32,128]{1,0:T(8,128)} %param.13) | copy-start | bytes 49156
  0.0 24.4 %copy-start.5 = (f32[4,128,256]{2,1,0:T(8,128)S(1)}, f32[4,128,256]{2,1,0:T(8,128)}, u32[]{:S(2)}) copy-start(f32[4,128,256]{2,1,0:T(8,128)} %param.9) | copy-start | bytes 1572868
  0.0 24.4 %copy-start.7 = (f32[128,256]{1,0:T(8,128)S(1)}, f32[128,256]{1,0:T(8,128)}, u32[]{:S(2)}) copy-start(f32[128,256]{1,0:T(8,128)} %param.8) | copy-start | bytes 393220
  1.2 23.2 %collective-permute-start.1 = (f32[5,50,256]{2,1,0:T(8,128)S(1)}, f32[5,50,256]{2,1,0:T(8,128)S(1)}, u32[]{:S(2)}, u32[]{:S(2)}) collective-permute-start(f32[5,50,256]{2,1,0:T(8,128)S(1)} %get-tuple-element.456), channel_id=1, source_target_pairs={{4,0},{8,4},{12,8},{16,12},{20,16},{24,20},{28,24},{5,1},{9,5},{13... | collective-permute-start | bytes 768008 | tf_op jit(solution)/shard_map/ppermute | solution.py:29
  2.5 21.9 %collective-permute-start = (f32[5,50,256]{2,1,0:T(8,128)S(1)}, f32[5,50,256]{2,1,0:T(8,128)S(1)}, u32[]{:S(2)}, u32[]{:S(2)}) collective-permute-start(f32[5,50,256]{2,1,0:T(8,128)S(1)} %get-tuple-element.455), channel_id=1, source_target_pairs={{0,4},{4,8},{8,12},{12,16},{16,20},{20,24},{24,28},{1,5},{5,9},{9,... | collective-permute-start | bytes 768008 | tf_op jit(solution)/shard_map/ppermute | solution.py:28
  25.7 11.3 %collective-permute-start.3 = (f32[5,228,50]{1,2,0:T(8,128)}, f32[5,228,50]{1,2,0:T(8,128)S(1)}, u32[]{:S(2)}, u32[]{:S(2)}) collective-permute-start(f32[5,228,50]{1,2,0:T(8,128)} %copy.20), channel_id=1, source_target_pairs={{1,0},{2,1},{3,2},{5,4},{6,5},{7,6},{9,8},{10,9},{11,10},{13,12},{... | collective-permute-start | bytes 684008 | tf_op jit(solution)/shard_map/ppermute | solution.py:29
  27.3 11.9 %copy-start.8 = (f32[128,256]{1,0:T(8,128)S(1)}, f32[128,256]{1,0:T(8,128)}, u32[]{:S(2)}) copy-start(f32[128,256]{1,0:T(8,128)} %param.8) | copy-start | bytes 393220
  27.3 10.8 %collective-permute-start.2 = (f32[5,228,50]{1,2,0:T(8,128)S(1)}, f32[5,228,50]{1,2,0:T(8,128)S(1)}, u32[]{:S(2)}, u32[]{:S(2)}) collective-permute-start(f32[5,228,50]{1,2,0:T(8,128)S(1)} %copy.19), channel_id=1, source_target_pairs={{0,1},{1,2},{2,3},{4,5},{5,6},{6,7},{8,9},{9,10},{10,11},{12,13},{... | collective-permute-start | bytes 684008 | tf_op jit(solution)/shard_map/ppermute | solution.py:28
  61.0 5.7 %copy-start.1 = (f32[5,138,311]{2,1,0:T(8,128)}, f32[5,138,311]{2,1,0:T(8,128)S(1)}, u32[]{:S(2)}) copy-start(f32[5,138,311]{2,1,0:T(8,128)S(1)} %get-tuple-element.604) | copy-start | bytes 2575084 | tf_op jit(solution)/shard_map/while
  74.3 5.7 %copy-start.1 = (f32[5,138,311]{2,1,0:T(8,128)}, f32[5,138,311]{2,1,0:T(8,128)S(1)}, u32[]{:S(2)}) copy-start(f32[5,138,311]{2,1,0:T(8,128)S(1)} %get-tuple-element.604) | copy-start | bytes 2575084 | tf_op jit(solution)/shard_map/while
  80.0 3.7 %copy-start.3 = (f32[5,128,301]{2,1,0:T(8,128)S(1)}, f32[5,128,301]{2,1,0:T(8,128)}, u32[]{:S(2)}) copy-start(f32[5,128,301]{2,1,0:T(8,128)} %get-tuple-element.609) | copy-start | bytes 2311684 | tf_op jit(solution)/shard_map/while
  80.0 3.7 %copy-start.4 = (f32[5,128,301]{2,1,0:T(8,128)S(1)}, f32[5,128,301]{2,1,0:T(8,128)}, u32[]{:S(2)}) copy-start(f32[5,128,301]{2,1,0:T(8,128)} %get-tuple-element.607) | copy-start | bytes 2311684 | tf_op jit(solution)/shard_map/while
  87.6 5.7 %copy-start.1 = (f32[5,138,311]{2,1,0:T(8,128)}, f32[5,138,311]{2,1,0:T(8,128)S(1)}, u32[]{:S(2)}) copy-start(f32[5,138,311]{2,1,0:T(8,128)S(1)} %get-tuple-element.604) | copy-start | bytes 2575084 | tf_op jit(solution)/shard_map/while
  93.3 3.7 %copy-start.3 = (f32[5,128,301]{2,1,0:T(8,128)S(1)}, f32[5,128,301]{2,1,0:T(8,128)}, u32[]{:S(2)}) copy-start(f32[5,128,301]{2,1,0:T(8,128)} %get-tuple-element.609) | copy-start | bytes 2311684 | tf_op jit(solution)/shard_map/while
  93.3 3.7 %copy-start.4 = (f32[5,128,301]{2,1,0:T(8,128)S(1)}, f32[5,128,301]{2,1,0:T(8,128)}, u32[]{:S(2)}) copy-start(f32[5,128,301]{2,1,0:T(8,128)} %get-tuple-element.607) | copy-start | bytes 2311684 | tf_op jit(solution)/shard_map/while
  100.9 5.7 %copy-start.1 = (f32[5,138,311]{2,1,0:T(8,128)}, f32[5,138,311]{2,1,0:T(8,128)S(1)}, u32[]{:S(2)}) copy-start(f32[5,138,311]{2,1,0:T(8,128)S(1)} %get-tuple-element.604) | copy-start | bytes 2575084 | tf_op jit(solution)/shard_map/while
  106.6 3.7 %copy-start.3 = (f32[5,128,301]{2,1,0:T(8,128)S(1)}, f32[5,128,301]{2,1,0:T(8,128)}, u32[]{:S(2)}) copy-start(f32[5,128,301]{2,1,0:T(8,128)} %get-tuple-element.609) | copy-start | bytes 2311684 | tf_op jit(solution)/shard_map/while
  106.6 3.7 %copy-start.4 = (f32[5,128,301]{2,1,0:T(8,128)S(1)}, f32[5,128,301]{2,1,0:T(8,128)}, u32[]{:S(2)}) copy-start(f32[5,128,301]{2,1,0:T(8,128)} %get-tuple-element.607) | copy-start | bytes 2311684 | tf_op jit(solution)/shard_map/while
  114.2 5.7 %copy-start.1 = (f32[5,138,311]{2,1,0:T(8,128)}, f32[5,138,311]{2,1,0:T(8,128)S(1)}, u32[]{:S(2)}) copy-start(f32[5,138,311]{2,1,0:T(8,128)S(1)} %get-tuple-element.604) | copy-start | bytes 2575084 | tf_op jit(solution)/shard_map/while
  119.9 3.7 %copy-start.3 = (f32[5,128,301]{2,1,0:T(8,128)S(1)}, f32[5,128,301]{2,1,0:T(8,128)}, u32[]{:S(2)}) copy-start(f32[5,128,301]{2,1,0:T(8,128)} %get-tuple-element.609) | copy-start | bytes 2311684 | tf_op jit(solution)/shard_map/while
  119.9 3.7 %copy-start.4 = (f32[5,128,301]{2,1,0:T(8,128)S(1)}, f32[5,128,301]{2,1,0:T(8,128)}, u32[]{:S(2)}) copy-start(f32[5,128,301]{2,1,0:T(8,128)} %get-tuple-element.607) | copy-start | bytes 2311684 | tf_op jit(solution)/shard_map/while
  127.5 5.7 %copy-start.1 = (f32[5,138,311]{2,1,0:T(8,128)}, f32[5,138,311]{2,1,0:T(8,128)S(1)}, u32[]{:S(2)}) copy-start(f32[5,138,311]{2,1,0:T(8,128)S(1)} %get-tuple-element.604) | copy-start | bytes 2575084 | tf_op jit(solution)/shard_map/while
  133.2 3.7 %copy-start.3 = (f32[5,128,301]{2,1,0:T(8,128)S(1)}, f32[5,128,301]{2,1,0:T(8,128)}, u32[]{:S(2)}) copy-start(f32[5,128,301]{2,1,0:T(8,128)} %get-tuple-element.609) | copy-start | bytes 2311684 | tf_op jit(solution)/shard_map/while
  133.2 3.7 %copy-start.4 = (f32[5,128,301]{2,1,0:T(8,128)S(1)}, f32[5,128,301]{2,1,0:T(8,128)}, u32[]{:S(2)}) copy-start(f32[5,128,301]{2,1,0:T(8,128)} %get-tuple-element.607) | copy-start | bytes 2311684 | tf_op jit(solution)/shard_map/while
  140.8 5.7 %copy-start.1 = (f32[5,138,311]{2,1,0:T(8,128)}, f32[5,138,311]{2,1,0:T(8,128)S(1)}, u32[]{:S(2)}) copy-start(f32[5,138,311]{2,1,0:T(8,128)S(1)} %get-tuple-element.604) | copy-start | bytes 2575084 | tf_op jit(solution)/shard_map/while
  146.5 3.7 %copy-start.3 = (f32[5,128,301]{2,1,0:T(8,128)S(1)}, f32[5,128,301]{2,1,0:T(8,128)}, u32[]{:S(2)}) copy-start(f32[5,128,301]{2,1,0:T(8,128)} %get-tuple-element.609) | copy-start | bytes 2311684 | tf_op jit(solution)/shard_map/while
  146.5 3.7 %copy-start.4 = (f32[5,128,301]{2,1,0:T(8,128)S(1)}, f32[5,128,301]{2,1,0:T(8,128)}, u32[]{:S(2)}) copy-start(f32[5,128,301]{2,1,0:T(8,128)} %get-tuple-element.607) | copy-start | bytes 2311684 | tf_op jit(solution)/shard_map/while
  154.1 5.7 %copy-start.1 = (f32[5,138,311]{2,1,0:T(8,128)}, f32[5,138,311]{2,1,0:T(8,128)S(1)}, u32[]{:S(2)}) copy-start(f32[5,138,311]{2,1,0:T(8,128)S(1)} %get-tuple-element.604) | copy-start | bytes 2575084 | tf_op jit(solution)/shard_map/while
  159.8 3.7 %copy-start.3 = (f32[5,128,301]{2,1,0:T(8,128)S(1)}, f32[5,128,301]{2,1,0:T(8,128)}, u32[]{:S(2)}) copy-start(f32[5,128,301]{2,1,0:T(8,128)} %get-tuple-element.609) | copy-start | bytes 2311684 | tf_op jit(solution)/shard_map/while
  159.8 3.7 %copy-start.4 = (f32[5,128,301]{2,1,0:T(8,128)S(1)}, f32[5,128,301]{2,1,0:T(8,128)}, u32[]{:S(2)}) copy-start(f32[5,128,301]{2,1,0:T(8,128)} %get-tuple-element.607) | copy-start | bytes 2311684 | tf_op jit(solution)/shard_map/while
  167.4 5.7 %copy-start.1 = (f32[5,138,311]{2,1,0:T(8,128)}, f32[5,138,311]{2,1,0:T(8,128)S(1)}, u32[]{:S(2)}) copy-start(f32[5,138,311]{2,1,0:T(8,128)S(1)} %get-tuple-element.604) | copy-start | bytes 2575084 | tf_op jit(solution)/shard_map/while
  173.1 3.7 %copy-start.3 = (f32[5,128,301]{2,1,0:T(8,128)S(1)}, f32[5,128,301]{2,1,0:T(8,128)}, u32[]{:S(2)}) copy-start(f32[5,128,301]{2,1,0:T(8,128)} %get-tuple-element.609) | copy-start | bytes 2311684 | tf_op jit(solution)/shard_map/while
  173.1 3.7 %copy-start.4 = (f32[5,128,301]{2,1,0:T(8,128)S(1)}, f32[5,128,301]{2,1,0:T(8,128)}, u32[]{:S(2)}) copy-start(f32[5,128,301]{2,1,0:T(8,128)} %get-tuple-element.607) | copy-start | bytes 2311684 | tf_op jit(solution)/shard_map/while
  180.7 5.7 %copy-start.1 = (f32[5,138,311]{2,1,0:T(8,128)}, f32[5,138,311]{2,1,0:T(8,128)S(1)}, u32[]{:S(2)}) copy-start(f32[5,138,311]{2,1,0:T(8,128)S(1)} %get-tuple-element.604) | copy-start | bytes 2575084 | tf_op jit(solution)/shard_map/while
  186.4 3.7 %copy-start.3 = (f32[5,128,301]{2,1,0:T(8,128)S(1)}, f32[5,128,301]{2,1,0:T(8,128)}, u32[]{:S(2)}) copy-start(f32[5,128,301]{2,1,0:T(8,128)} %get-tuple-element.609) | copy-start | bytes 2311684 | tf_op jit(solution)/shard_map/while
  186.4 3.7 %copy-start.4 = (f32[5,128,301]{2,1,0:T(8,128)S(1)}, f32[5,128,301]{2,1,0:T(8,128)}, u32[]{:S(2)}) copy-start(f32[5,128,301]{2,1,0:T(8,128)} %get-tuple-element.607) | copy-start | bytes 2311684 | tf_op jit(solution)/shard_map/while
  194.0 5.7 %copy-start.1 = (f32[5,138,311]{2,1,0:T(8,128)}, f32[5,138,311]{2,1,0:T(8,128)S(1)}, u32[]{:S(2)}) copy-start(f32[5,138,311]{2,1,0:T(8,128)S(1)} %get-tuple-element.604) | copy-start | bytes 2575084 | tf_op jit(solution)/shard_map/while
  207.3 5.7 %copy-start.1 = (f32[5,138,311]{2,1,0:T(8,128)}, f32[5,138,311]{2,1,0:T(8,128)S(1)}, u32[]{:S(2)}) copy-start(f32[5,138,311]{2,1,0:T(8,128)S(1)} %get-tuple-element.604) | copy-start | bytes 2575084 | tf_op jit(solution)/shard_map/while
  220.6 5.7 %copy-start.1 = (f32[5,138,311]{2,1,0:T(8,128)}, f32[5,138,311]{2,1,0:T(8,128)S(1)}, u32[]{:S(2)}) copy-start(f32[5,138,311]{2,1,0:T(8,128)S(1)} %get-tuple-element.604) | copy-start | bytes 2575084 | tf_op jit(solution)/shard_map/while
  233.9 5.7 %copy-start.1 = (f32[5,138,311]{2,1,0:T(8,128)}, f32[5,138,311]{2,1,0:T(8,128)S(1)}, u32[]{:S(2)}) copy-start(f32[5,138,311]{2,1,0:T(8,128)S(1)} %get-tuple-element.604) | copy-start | bytes 2575084 | tf_op jit(solution)/shard_map/while
  247.2 5.7 %copy-start.1 = (f32[5,138,311]{2,1,0:T(8,128)}, f32[5,138,311]{2,1,0:T(8,128)S(1)}, u32[]{:S(2)}) copy-start(f32[5,138,311]{2,1,0:T(8,128)S(1)} %get-tuple-element.604) | copy-start | bytes 2575084 | tf_op jit(solution)/shard_map/while
  260.5 5.7 %copy-start.1 = (f32[5,138,311]{2,1,0:T(8,128)}, f32[5,138,311]{2,1,0:T(8,128)S(1)}, u32[]{:S(2)}) copy-start(f32[5,138,311]{2,1,0:T(8,128)S(1)} %get-tuple-element.604) | copy-start | bytes 2575084 | tf_op jit(solution)/shard_map/while
  273.8 15.1 %copy-start.11 = (f32[128,256]{1,0:T(8,128)S(1)}, f32[128,256]{1,0:T(8,128)}, u32[]{:S(2)}) copy-start(f32[128,256]{1,0:T(8,128)} %fusion.86) | copy-start | bytes 393220
  275.2 4.4 %collective-permute-start.5 = (f32[1,256]{1,0:T(1,128)S(1)}, f32[1,256]{1,0:T(1,128)S(1)}, u32[]{:S(2)}, u32[]{:S(2)}) collective-permute-start(f32[1,256]{1,0:T(1,128)S(1)} %get-tuple-element.460), channel_id=1, source_target_pairs={{4,0},{8,4},{12,8},{16,12},{20,16},{24,20},{28,24},{5,1},{9,5},{13... | collective-permute-start | bytes 3080 | tf_op jit(solution)/shard_map/ppermute | solution.py:29
  276.5 3.8 %collective-permute-start.4 = (f32[1,256]{1,0:T(1,128)S(1)}, f32[1,256]{1,0:T(1,128)S(1)}, u32[]{:S(2)}, u32[]{:S(2)}) collective-permute-start(f32[1,256]{1,0:T(1,128)S(1)} %get-tuple-element.459), channel_id=1, source_target_pairs={{0,4},{4,8},{8,12},{12,16},{16,20},{20,24},{24,28},{1,5},{5,9},{9,... | collective-permute-start | bytes 3080 | tf_op jit(solution)/shard_map/ppermute | solution.py:28
  280.5 6.6 %collective-permute-start.7 = (f32[130,1]{1,0:T(8,128)S(1)}, f32[130,1]{1,0:T(8,128)S(1)}, u32[]{:S(2)}, u32[]{:S(2)}) collective-permute-start(f32[130,1]{1,0:T(8,128)S(1)} %get-tuple-element.458), channel_id=1, source_target_pairs={{1,0},{2,1},{3,2},{5,4},{6,5},{7,6},{9,8},{10,9},{11,10},{13,12},{... | collective-permute-start | bytes 1568 | tf_op jit(solution)/shard_map/ppermute | solution.py:29
  281.8 7.1 %collective-permute-start.6 = (f32[130,1]{1,0:T(8,128)S(1)}, f32[130,1]{1,0:T(8,128)S(1)}, u32[]{:S(2)}, u32[]{:S(2)}) collective-permute-start(f32[130,1]{1,0:T(8,128)S(1)} %get-tuple-element.457), channel_id=1, source_target_pairs={{0,1},{1,2},{2,3},{4,5},{5,6},{6,7},{8,9},{9,10},{10,11},{12,13},{... | collective-permute-start | bytes 1568 | tf_op jit(solution)/shard_map/ppermute | solution.py:28
  (35 other events, 84.8 us)
where the time goes:
time: 296 us; the launch traced here: 290 us
  matrix products  69.1 us (23%)
  other arithmetic  67.5 us (23%)
  local copies, waits for them, and re-layouts  65.2 us (22%)
  loops' own time  42.4 us (14%)
  starting transfers between devices  20.5 us (7%)
  blocking collectives  17.9 us (6%)
  waiting for transfers between devices  7.22 us (2%)
    another operation x1, loops' own time, on_device(): lax.fori_loop(0, LEVELS, level_step, jnp.zeros((HYP, rows_tile, cols_tile...  42.4 us
    dot_general x17, matrix products, window_box(): jnp.einsum('ij,mjk->mik', row_band, maps, precision=lax.Precision.HIGHEST)  42.3 us
    broadcast_in_dim x16, other arithmetic, level_step(): jnp.where(hypotheses == depth_level, volume[None], 0.0)  26.4 us
    dot_general x17, matrix products, window_box(): jnp.einsum('mik,lk->mil', summed, col_band, precision=lax.Precision.HIGHEST)  25.4 us
    mul x16, other arithmetic, level_step(): elementwise_multiples.append(ref_window * src_window)  25.3 us
    ppermute x4, starting transfers between devices, extended_2(): before = lax.ppermute(last, axis, up)  15.3 us
    slice x16, local copies, waits for them, and re-layouts, level_step(): wide_mean[view_slot + 1]  14.8 us
    slice x16, local copies, waits for them, and re-layouts, level_step(): extended[view_slot + 1]  14.5 us
  transfers between devices with their start and end apart: 8, of which 4 were waited for; matrix products, arithmetic and copies ran while one was open for 1% of the time, Pallas kernels for 0%

commit v1 on v0

v1 whole, which is shorter than its diff:
```python
import functools

import jax
import jax.numpy as jnp
from jax import lax
from jax.experimental import pallas as pl
from jax.experimental.pallas import tpu as pltpu
from jax.sharding import PartitionSpec as P

LEVELS = 16
HYP = 8
SRC = 4
MAXID = 3
WIN = 11
UPS = 8
CITER = 4
RAD = WIN // 2
LANES = 128
Q = 8
EDGE = 8
PADC = 8
LEFT = -(-(MAXID * (LEVELS - 1) + RAD) // 8) * 8
MLEFT = -(-(MAXID * (LEVELS - 1)) // 8) * 8

FLOOR = 1e-05
AREA = float(WIN * WIN)
F32 = jnp.float32
BF16 = jnp.bfloat16
MESH = pl.DeviceIdType.MESH


def col_box(p, n):
    s2 = p[: n + 9] + p[1 : n + 10]
    s4 = s2[: n + 7] + s2[2 : n + 9]
    s8 = s4[:n] + s4[4 : n + 4]
    return s8 + s2[8 : n + 8] + p[10 : n + 10]


def split3(y):
    y = y.reshape(-1, LANES)
    hi = y.astype(BF16)
    rest = y - hi.astype(F32)
    mid = rest.astype(BF16)
    low = (rest - mid.astype(F32)).astype(BF16)
    return hi, mid, low


def row_box(main, extra, weight):
    out = None
    for m, e in zip(main, extra):
        d = jnp.dot(jnp.concatenate([m, e], 1), weight, preferred_element_type=F32)
        out = d if out is None else out + d
    return out.reshape(-1, Q, LANES)


def interp_pair(fine, total):
    num = 2 * fine + (1 - UPS)
    shift = (2 * UPS).bit_length() - 1
    lower = lax.shift_right_arithmetic(num, jnp.full_like(num, shift))
    frac = (num - lower * (2 * UPS)).astype(F32) * (1.0 / (2 * UPS))
    lo = jnp.clip(lower, 0, total - 1)
    hi = jnp.clip(lower + 1, 0, total - 1)
    return lo, hi, frac


def iota(shape, dim):
    return lax.broadcasted_iota(jnp.int32, shape, dim)


def kernel(nr, nc, ids, ref, src, hyp, cd_ref, cc_ref, out, xt, up, down, corner, xe, ov, ove,
           mom, rmom, sel, cand, disp, conf, band, redt, redrow, edge, ups, work, send, recv):
    rows, cols = ref.shape
    tt = cols // Q
    r, c = lax.axis_index("row"), lax.axis_index("col")
    block = cd_ref.shape[0]
    ncr, ncc = block * nc, cd_ref.shape[1]
    ct = rows // UPS
    uu = LEFT + tt + EDGE
    ww = MLEFT + tt

    def peer(dr, dc):
        return {"row": lax.rem(r + dr + nr, nr), "col": lax.rem(c + dc + nc, nc)}

    offsets = sorted(
        {(dr % nr, dc % nc) for dr in (-1, 0, 1) for dc in (-1, 0, 1)}
        | {(0, dc) for dc in range(nc)}
    )
    offsets = [o for o in offsets if o != (0, 0)]
    barrier = pltpu.get_barrier_semaphore()
    for dr, dc in offsets:
        pl.semaphore_signal(barrier, inc=1, device_id=peer(dr, dc), device_id_type=MESH)

    zero_pad = jnp.zeros((PADC, ncc), F32)
    for grid_ref in (disp, conf):
        grid_ref[0:PADC] = zero_pad
        grid_ref[PADC + ncr : 2 * PADC + ncr] = zero_pad
    mine = pl.multiple_of(PADC + block * c, 8)
    disp[pl.ds(mine, block)] = cd_ref[...]
    conf[pl.ds(mine, block)] = cc_ref[...]
    pl.semaphore_wait(barrier, len(offsets))

    copies = []

    def push(a, b, dr, dc):
        k = len(copies)
        copy = pltpu.make_async_remote_copy(
            src_ref=a, dst_ref=b, send_sem=send.at[k], recv_sem=recv.at[k],
            device_id=peer(dr, dc), device_id_type=MESH,
        )
        copy.start()
        copies.append(copy)
        return copy

    last = rows - EDGE
    near = []
    for dr, lo, dst in ((-1, 0, down), (1, last, up)):
        near.append(push(ref.at[pl.ds(lo, EDGE)], dst.at[0], dr, 0))
        near.append(push(src.at[:, pl.ds(lo, EDGE)], dst.at[pl.ds(1, SRC)], dr, 0))
    for dr, lo, vert in ((-1, 0, 1), (1, last, 0)):
        for dc, cl, side in ((-1, 0, 1), (1, cols - LANES, 0)):
            dst = corner.at[vert, side]
            near.append(push(ref.at[pl.ds(lo, EDGE), pl.ds(cl, LANES)], dst.at[0], dr, dc))
            near.append(push(
                src.at[:, pl.ds(lo, EDGE), pl.ds(cl, LANES)], dst.at[pl.ds(1, SRC)], dr, dc
            ))
    for a in range(SRC + 1):
        image = ref[...] if a == 0 else src[a - 1]
        xt[a, LEFT : LEFT + cols] = image.T
    strips = [
        push(xt.at[:, pl.ds(cols, LEFT)], xt.at[:, pl.ds(0, LEFT)], 0, 1),
        push(xt.at[:, pl.ds(LEFT, EDGE)], xt.at[:, pl.ds(LEFT + cols, EDGE)], 0, -1),
    ]
    coarse = []
    for o in range(1, nc):
        for a, b in ((cd_ref, disp), (cc_ref, conf)):
            coarse.append(push(a, b.at[pl.ds(mine, block)], 0, o))

    def hyp_step(k, carry):
        work[...] = hyp[k].astype(F32).T
        for t in range(tt):
            cand[k, t] = work[pl.ds(t, Q, stride=tt), :]
        return carry

    lax.fori_loop(0, HYP, hyp_step, 0)

    kk = iota((2 * LANES, LANES), 0)
    oo = iota((2 * LANES, LANES), 1)
    for v in range(SRC):
        e = kk - LANES - 2 * EDGE * v
        pos = jnp.where(kk < LANES, kk, jnp.where(e < EDGE, e - EDGE, LANES + e - EDGE))
        ok = (jnp.abs(pos - oo) <= RAD) & ((kk < LANES) | ((e >= 0) & (e < 2 * EDGE)))
        band[v] = jnp.where(ok, 1.0, 0.0).astype(BF16)

    for copy in coarse:
        copy.wait()
    win = ct + 2 * PADC
    start = pl.multiple_of(ct * r, 8)
    d0 = disp[pl.ds(start, win)]
    f0 = conf[pl.ds(start, win)]
    grid_row = iota((win, ncc), 0) + (ct * r - PADC)
    valid = (grid_row >= 0) & (grid_row < ncr)
    lane = iota((win, ncc), 1)
    inv = jnp.where(valid, 1.0 / (f0 + 4.0), 0.0)
    base = f0 * d0
    cur = d0
    for _ in range(CITER):
        nb = pltpu.roll(cur, 1, 0) + pltpu.roll(cur, win - 1, 0)
        nb = nb + jnp.where(lane == 0, 0.0, pltpu.roll(cur, 1, 1))
        nb = nb + jnp.where(lane == ncc - 1, 0.0, pltpu.roll(cur, ncc - 1, 1))
        cur = (base + nb) * inv
    m = iota((cols, ncc), 0)
    lo, hi, frac = interp_pair(c * cols + lax.rem(m, Q) * tt + lax.div(m, Q), ncc)
    cl = iota((cols, ncc), 1)
    cmat = jnp.where(cl == lo, 1.0 - frac, 0.0) + jnp.where(cl == hi, frac, 0.0)
    lo, hi, frac = interp_pair(r * rows + iota((win, rows), 1), ncr)
    rl = iota((win, rows), 0) + (ct * r - PADC)
    rmat = jnp.where(rl == lo, 1.0 - frac, 0.0) + jnp.where(rl == hi, frac, 0.0)
    wide = lax.dot_general(
        cmat, cur, (((1,), (1,)), ((), ())), precision=lax.Precision.HIGHEST,
        preferred_element_type=F32,
    )
    ups[...] = jnp.dot(
        wide, rmat, precision=lax.Precision.HIGHEST, preferred_element_type=F32
    ).reshape(tt, Q, LANES)

    for copy in near:
        copy.wait()
    top, bottom, lside, rside = r > 0, r < nr - 1, c > 0, c < nc - 1

    def halo_rows(get_up, get_down, ok):
        for w in range(2):
            parts = []
            for v in range(SRC):
                a = 0 if w == 0 else v + 1
                parts.append(jnp.where(top & ok, get_up(a), 0.0))
                parts.append(jnp.where(bottom & ok, get_down(a), 0.0))
            parts.append(jnp.zeros((LANES - 2 * EDGE * SRC, LANES), F32))
            yield w, jnp.concatenate(parts, 0).T

    for b in range(cols // LANES):
        s = b * LANES
        for w, x in halo_rows(
            lambda a: up[a, :, s : s + LANES], lambda a: down[a, :, s : s + LANES], True
        ):
            xe[w, LEFT + s : LEFT + s + LANES] = x
    for w, x in halo_rows(lambda a: corner[0, 0, a], lambda a: corner[1, 0, a], lside):
        xe[w, 0:LEFT] = x[LANES - LEFT :]
    for w, x in halo_rows(lambda a: corner[0, 1, a], lambda a: corner[1, 1, a], rside):
        xe[w, LEFT + cols : LEFT + cols + EDGE] = x[:EDGE]
    for copy in strips:
        copy.wait()

    @pl.when(c == 0)
    def _():
        xt[:, 0:LEFT] = jnp.zeros((SRC + 1, LEFT, LANES), F32)

    @pl.when(c == nc - 1)
    def _():
        xt[:, LEFT + cols : LEFT + cols + EDGE] = jnp.zeros((SRC + 1, EDGE, LANES), F32)

    def spread(b, carry):
        for k in range(8):
            u = b * 8 + k
            for a in range(SRC + 1):
                ov[a, u] = xt[a, pl.ds(u, Q, stride=tt), :]
            for w in range(2):
                ove[w, u] = xe[w, pl.ds(u, Q, stride=tt), :]
        return carry

    lax.fori_loop(0, uu // 8, spread, 0)

    def mean_and_scale(x, e, n, v):
        means = row_box(split3(col_box(x, n)), e[0], band[v]) * (1.0 / AREA)
        squares = row_box(split3(col_box(x * x, n)), e[1], band[v]) * (1.0 / AREA)
        return means, lax.rsqrt(squares - means * means + FLOOR)

    mb = 16
    off = LEFT - RAD

    def ref_moments(b, carry):
        at = b * mb
        x = ov[0, pl.ds(off + at, mb + WIN - 1)]
        e = ove[0, pl.ds(off + at, mb + WIN - 1)]
        es = split3(col_box(e, mb)), split3(col_box(e * e, mb))
        mean, scale = mean_and_scale(x, es, mb, 0)
        rmom[0, pl.ds(at, mb)] = mean
        rmom[1, pl.ds(at, mb)] = scale * (1.0 / SRC)
        return carry

    lax.fori_loop(0, tt // mb, ref_moments, 0)

    def src_moments(b, carry):
        at = b * mb
        u = at + off - MLEFT
        e = ove[1, pl.ds(u, mb + WIN - 1)]
        es = split3(col_box(e, mb)), split3(col_box(e * e, mb))
        for v in range(SRC):
            x = ov[v + 1, pl.ds(u, mb + WIN - 1)]
            mean, scale = mean_and_scale(x, es, mb, v)
            mom[v, 0, pl.ds(at, mb)] = mean
            mom[v, 1, pl.ds(at, mb)] = scale
        return carry

    lax.fori_loop(0, ww // mb, src_moments, 0)

    sel[...] = jnp.zeros(sel.shape, F32)
    group = lax.shift_right_logical(iota((1, Q, LANES), 2), jnp.full((1, Q, LANES), 4))
    tb = 16
    span = tb + WIN - 1

    def level(i, carry):
        depth = lax.div(i, tt // tb)
        at = lax.rem(i, tt // tb) * tb
        moved = [ids[v] * depth for v in range(SRC)]
        e = ove[1, pl.ds(off + at - moved[0], span)]
        for v in range(1, SRC):
            e = jnp.where(group == v, ove[1, pl.ds(off + at - moved[v], span)], e)
        es = split3(col_box(e * ove[0, pl.ds(off + at, span)], tb))
        x0 = ov[0, pl.ds(off + at, span)]
        mr = rmom[0, pl.ds(at, tb)]
        total = None
        for v in range(SRC):
            y = col_box(x0 * ov[v + 1, pl.ds(off + at - moved[v], span)], tb)
            cross = row_box(split3(y), es, band[v]) * (1.0 / AREA)
            wi = MLEFT + at - moved[v]
            part = (cross - mr * mom[v, 0, pl.ds(wi, tb)]) * mom[v, 1, pl.ds(wi, tb)]
            total = part if total is None else total + part
        volume = total * rmom[1, pl.ds(at, tb)]
        depth_f = depth.astype(F32)
        for k in range(HYP):
            sel[k, pl.ds(at, tb)] = jnp.where(
                cand[k, pl.ds(at, tb)] == depth_f, volume, sel[k, pl.ds(at, tb)]
            )
        return carry

    lax.fori_loop(0, LEVELS * (tt // tb), level, 0)

    def estimate(at, n, centre):
        num = den = None
        for k in range(HYP):
            ck = cand[k, pl.ds(at, n)]
            diff = ck - centre
            wt = jnp.exp((sel[k, pl.ds(at, n)] - 1.0 - 0.01 * diff * diff) * 10.0)
            num = wt * ck if num is None else num + wt * ck
            den = wt if den is None else den + wt
        return num / den

    eb = 8

    def red_step(b, carry):
        at = b * eb
        red = estimate(at, eb, ups[pl.ds(at, eb)])
        for k in range(eb):
            redt[pl.ds(EDGE + at + k, Q, stride=tt), :] = red[k]
        return carry

    lax.fori_loop(0, tt // eb, red_step, 0)
    redrow[0] = redt[EDGE : EDGE + cols, :].T[0:EDGE]
    redrow[1] = redt[EDGE : EDGE + cols, :].T[last:rows]
    borders = [
        push(redt.at[pl.ds(EDGE, EDGE)], redt.at[pl.ds(EDGE + cols, EDGE)], 0, -1),
        push(redt.at[pl.ds(cols, EDGE)], redt.at[pl.ds(0, EDGE)], 0, 1),
        push(redrow.at[0], redrow.at[3], -1, 0),
        push(redrow.at[1], redrow.at[2], 1, 0),
    ]
    for copy in borders:
        copy.wait()
    row_no = iota((rows, cols), 0)
    above = jnp.where(top, redrow[2][EDGE - 1 : EDGE], 0.0)
    below = jnp.where(bottom, redrow[3][0:1], 0.0)
    edge[...] = jnp.where(row_no == 0, above, jnp.where(row_no == rows - 1, below, 0.0)).T

    @pl.when(c == 0)
    def _():
        redt[0:EDGE] = jnp.zeros((EDGE, LANES), F32)

    @pl.when(c == nc - 1)
    def _():
        redt[EDGE + cols : 2 * EDGE + cols] = jnp.zeros((EDGE, LANES), F32)

    lane2 = iota((Q, LANES), 1)
    chunk = iota((Q, LANES), 0)
    gi = r * rows + lane2
    rcount = 4.0 - jnp.where(gi == 0, 1.0, 0.0) - jnp.where(gi == nr * rows - 1, 1.0, 0.0)

    def black_step(t, carry):
        red = redt[pl.ds(EDGE + t, Q, stride=tt), :]
        nb = redt[pl.ds(EDGE - 1 + t, Q, stride=tt), :] + redt[pl.ds(EDGE + 1 + t, Q, stride=tt), :]
        nb = nb + jnp.where(lane2 == 0, 0.0, pltpu.roll(red, 1, 1))
        nb = nb + jnp.where(lane2 == LANES - 1, 0.0, pltpu.roll(red, LANES - 1, 1))
        nb = nb + edge[pl.ds(t, Q, stride=tt), :]
        gj = c * cols + chunk * tt + t
        count = rcount - jnp.where(gj == 0, 1.0, 0.0) - jnp.where(gj == nc * cols - 1, 1.0, 0.0)
        centre = 0.5 * ups[t] + 0.5 * nb / count
        black = estimate(t, 1, centre[None])[0]
        even = lax.rem(gi + gj, 2) == 0
        work[pl.ds(t, Q, stride=tt), :] = jnp.where(even, red, black)
        return carry

    lax.fori_loop(0, tt, black_step, 0)
    out[...] = work[...].T


def on_device(nr, nc, reference_image, source_images, hypotheses, source_ids, disp, conf):
    rows, cols = reference_image.shape
    tt = cols // Q
    block, ncc = disp.shape
    uu = LEFT + tt + EDGE
    ww = MLEFT + tt
    full = LEFT + cols + EDGE
    count = 4 + 8 + 2 + 2 * (nc - 1) + 4
    v = lambda *s: pltpu.VMEM(s, F32)
    vmem = pl.BlockSpec(memory_space=pltpu.VMEM)
    return pl.pallas_call(
        functools.partial(kernel, nr, nc),
        out_shape=jax.ShapeDtypeStruct((rows, cols), F32),
        in_specs=[pl.BlockSpec(memory_space=pltpu.SMEM)] + [vmem] * 5,
        out_specs=vmem,
        scratch_shapes=[
            v(SRC + 1, full, LANES),
            v(SRC + 1, EDGE, cols),
            v(SRC + 1, EDGE, cols),
            v(2, 2, SRC + 1, EDGE, LANES),
            v(2, full, LANES),
            v(SRC + 1, uu, Q, LANES),
            v(2, uu, Q, LANES),
            v(SRC, 2, ww, Q, LANES),
            v(2, tt, Q, LANES),
            v(HYP, tt, Q, LANES),
            v(HYP, tt, Q, LANES),
            v(block * nc + 2 * PADC, ncc),
            v(block * nc + 2 * PADC, ncc),
            pltpu.VMEM((SRC, 2 * LANES, LANES), BF16),
            v(cols + 2 * EDGE, LANES),
            v(4, EDGE, cols),
            v(cols, LANES),
            v(tt, Q, LANES),
            v(cols, LANES),
            pltpu.SemaphoreType.DMA((count,)),
            pltpu.SemaphoreType.DMA((count,)),
        ],
        compiler_params=pltpu.CompilerParams(
            collective_id=0, has_side_effects=True, vmem_limit_bytes=48 * 1024 * 1024
        ),
        name="stereo",
    )(source_ids, reference_image, source_images, hypotheses, disp, conf)


def solution(mesh):
    nr, nc = mesh.shape["row"], mesh.shape["col"]
    in_specs = (
        P("row", "col"),
        P(None, "row", "col"),
        P(None, "row", "col"),
        P(),
        P("col", None),
        P("col", None),
    )
    return jax.shard_map(
        functools.partial(on_device, nr, nc),
        mesh=mesh, in_specs=in_specs, out_specs=P("row", "col"), check_vma=False,
    )
```

time: 296 us -> 49.1 us (0.17); the launches traced: 290 us -> 48.7 us
  matrix products: 69.1 us -> 0 us
  other arithmetic: 67.5 us -> 0 us
  local copies, waits for them, and re-layouts: 65.2 us -> 5.92 us
  Pallas kernels: 0 us -> 42.8 us
  loops' own time: 42.4 us -> 0 us
  starting transfers between devices: 20.5 us -> 0 us
  blocking collectives: 17.9 us -> 0 us
  waiting for transfers between devices: 7.22 us -> 0 us
    dot_general x36 -> x0, matrix products: 69.1 us -> none  [the longest x17 42.3 us: window_box(): jnp.einsum('ij,mjk->mik', row_band, maps, precision=lax.Precision.HIGHEST)]
    pallas_call x0 -> x1, Pallas kernels: none -> 42.8 us  [on_device(): pl.pallas_call(functools.partial(kernel, nr, nc), out_shape=jax.ShapeDtyp...]
    another operation x1 -> x0, loops' own time: 42.4 us -> none  [on_device(): lax.fori_loop(0, LEVELS, level_step, jnp.zeros((HYP, rows_tile, cols_tile...]
    slice x56 -> x0, local copies, waits for them, and re-layouts: 42 us -> none  [the longest x16 14.8 us: level_step(): wide_mean[view_slot + 1]]
    mul x17 -> x0, other arithmetic: 27 us -> none  [the longest x16 25.3 us: level_step(): elementwise_multiples.append(ref_window * src_window)]
    broadcast_in_dim x16 -> x0, other arithmetic: 26.4 us -> none  [level_step(): jnp.where(hypotheses == depth_level, volume[None], 0.0)]
    ppermute x8 -> x0, starting transfers between devices: 20.5 us -> none  [the longest x4 15.3 us: extended_2(): before = lax.ppermute(last, axis, up)]
    all_gather x2 -> x0, blocking collectives: 17.9 us -> none  [the longest x1 9.72 us: on_device(): lax.all_gather(coarse_disp, 'col', axis=0, tiled=True)]
  transfers between devices with their start and end apart: 8 -> 0, of which waited for: 4 -> 0; matrix products, arithmetic and copies ran while one was open for 1% -> 0% of each run, Pallas kernels for 0% -> 0%
where the time goes in v1:
time: 49.1 us; the launch traced here: 48.7 us
  Pallas kernels  42.8 us (87%)
  local copies, waits for them, and re-layouts  5.92 us (12%)
    pallas_call x1, Pallas kernels, on_device(): pl.pallas_call(functools.partial(kernel, nr, nc), out_shape=jax.ShapeDtyp...  42.8 us
    unnamed x13, local copies, waits for them, and re-layouts  5.92 us

profile of v1, /device:TPU:0, one launch (start us, length us, event | category | flops | bytes accessed | tf_op | source)
XLA Modules:
  0.0 48.7 jit_solution(7292464767337093589)
XLA Ops:
  0.0 0.0 copy-start
  0.0 1.2 %copy-done = s32[8,128,256]{2,1,0:T(8,128)S(1)} copy-done((s32[8,128,256]{2,1,0:T(8,128)S(1)}, s32[8,128,256]{2,1,0:T(8,128)}, u32[]{:S(2)}) %copy-start) | copy-done | bytes 1048600
  1.2 0.0 copy-start.1
  1.2 1.0 %copy-done.1 = f32[4,128,256]{2,1,0:T(8,128)S(1)} copy-done((f32[4,128,256]{2,1,0:T(8,128)S(1)}, f32[4,128,256]{2,1,0:T(8,128)}, u32[]{:S(2)}) %copy-start.1) | copy-done | bytes 524312
  2.3 0.0 copy-start.2
  2.3 0.9 %copy-done.2 = f32[128,256]{1,0:T(8,128)S(1)} copy-done((f32[128,256]{1,0:T(8,128)S(1)}, f32[128,256]{1,0:T(8,128)}, u32[]{:S(2)}) %copy-start.2) | copy-done | bytes 131096
  3.2 0.0 copy-start.3
  3.2 0.7 %copy-done.3 = f32[32,128]{1,0:T(8,128)S(1)} copy-done((f32[32,128]{1,0:T(8,128)S(1)}, f32[32,128]{1,0:T(8,128)}, u32[]{:S(2)}) %copy-start.3) | copy-done | bytes 16408
  3.9 0.0 copy-start.4
  3.9 0.7 %copy-done.4 = f32[32,128]{1,0:T(8,128)S(1)} copy-done((f32[32,128]{1,0:T(8,128)S(1)}, f32[32,128]{1,0:T(8,128)}, u32[]{:S(2)}) %copy-start.4) | copy-done | bytes 16408
  4.6 0.0 copy-start.5
  4.6 0.7 %copy-done.5 = s32[4]{0:T(128)S(1)} copy-done((s32[4]{0:T(128)S(1)}, s32[4]{0:T(128)}, u32[]{:S(2)}) %copy-start.5) | copy-done | bytes 40
  5.3 42.8 %stereo.1 = f32[128,256]{1,0:T(8,128)S(1)} custom-call(s32[4]{0:T(128)S(1)} %copy-done.5, f32[128,256]{1,0:T(8,128)S(1)} %copy-done.2, f32[4,128,256]{2,1,0:T(8,128)S(1)} %copy-done.1, s32[8,128,256]{2,1,0:T(8,128)S(1)} %copy-done, f32[32,128]{1,0:T(8,128)S(1)} %copy-done.3, f32[32,128]{1,0:T(8,128)S(1)} %copy-done.4), custom_call_target="tpu_custom_call" | custom-call | tf_op jit(solution)/shard_map/stereo/pallas_call | solution.py:374
  48.1 0.7 %copy.8 = f32[128,256]{1,0:T(8,128)} copy(f32[128,256]{1,0:T(8,128)S(1)} %stereo.1) | data formatting | bytes 262144
Async XLA Ops:
  0.0 1.2 %copy-start = (s32[8,128,256]{2,1,0:T(8,128)S(1)}, s32[8,128,256]{2,1,0:T(8,128)}, u32[]{:S(2)}) copy-start(s32[8,128,256]{2,1,0:T(8,128)} %hyp.1) | copy-start | bytes 3145732
  1.2 1.0 %copy-start.1 = (f32[4,128,256]{2,1,0:T(8,128)S(1)}, f32[4,128,256]{2,1,0:T(8,128)}, u32[]{:S(2)}) copy-start(f32[4,128,256]{2,1,0:T(8,128)} %src.1) | copy-start | bytes 1572868
  2.3 0.9 %copy-start.2 = (f32[128,256]{1,0:T(8,128)S(1)}, f32[128,256]{1,0:T(8,128)}, u32[]{:S(2)}) copy-start(f32[128,256]{1,0:T(8,128)} %ref.1) | copy-start | bytes 393220
  3.2 0.7 %copy-start.3 = (f32[32,128]{1,0:T(8,128)S(1)}, f32[32,128]{1,0:T(8,128)}, u32[]{:S(2)}) copy-start(f32[32,128]{1,0:T(8,128)} %cd_ref.1) | copy-start | bytes 49156
  3.9 0.7 %copy-start.4 = (f32[32,128]{1,0:T(8,128)S(1)}, f32[32,128]{1,0:T(8,128)}, u32[]{:S(2)}) copy-start(f32[32,128]{1,0:T(8,128)} %cc_ref.1) | copy-start | bytes 49156
  4.6 0.7 %copy-start.5 = (s32[4]{0:T(128)S(1)}, s32[4]{0:T(128)}, u32[]{:S(2)}) copy-start(s32[4]{0:T(128)} %ids.1) | copy-start | bytes 52

commit v2 on v1

--- a/solution.py
+++ b/solution.py
@@ -46,10 +46,8 @@
 
 
 def row_box(main, extra, weight):
-    out = None
-    for m, e in zip(main, extra):
-        d = jnp.dot(jnp.concatenate([m, e], 1), weight, preferred_element_type=F32)
-        out = d if out is None else out + d
+    pieces = [x for pair in zip(main, extra) for x in pair]
+    out = jnp.dot(jnp.concatenate(pieces, 1), weight[...], preferred_element_type=F32)
     return out.reshape(-1, Q, LANES)
 
 
@@ -67,7 +65,7 @@
     return lax.broadcasted_iota(jnp.int32, shape, dim)
 
 
-def kernel(nr, nc, ids, ref, src, hyp, cd_ref, cc_ref, out, xt, up, down, corner, xe, ov, ove,
+def kernel(nr, nc, ids_h, ref_h, src_h, hyp_h, cd_ref, cc_ref, out, ids, ref, src, hyp, local, xt, up, down, corner, xe, ov, ove,
            mom, rmom, sel, cand, disp, conf, band, redt, redrow, edge, ups, work, send, recv):
     rows, cols = ref.shape
     tt = cols // Q
@@ -90,13 +88,16 @@
     for dr, dc in offsets:
         pl.semaphore_signal(barrier, inc=1, device_id=peer(dr, dc), device_id_type=MESH)
 
+    mine = pl.multiple_of(PADC + block * c, 8)
+    loads = []
+    for a, b in ((ref_h, ref), (src_h, src), (cd_ref, disp.at[pl.ds(mine, block)]),
+                 (cc_ref, conf.at[pl.ds(mine, block)]), (ids_h, ids), (hyp_h, hyp)):
+        loads.append(pltpu.make_async_copy(a, b, local.at[len(loads)]))
+        loads[-1].start()
     zero_pad = jnp.zeros((PADC, ncc), F32)
     for grid_ref in (disp, conf):
         grid_ref[0:PADC] = zero_pad
         grid_ref[PADC + ncr : 2 * PADC + ncr] = zero_pad
-    mine = pl.multiple_of(PADC + block * c, 8)
-    disp[pl.ds(mine, block)] = cd_ref[...]
-    conf[pl.ds(mine, block)] = cc_ref[...]
     pl.semaphore_wait(barrier, len(offsets))
 
     copies = []
@@ -114,26 +115,34 @@
     last = rows - EDGE
     near = []
     for dr, lo, dst in ((-1, 0, down), (1, last, up)):
-        near.append(push(ref.at[pl.ds(lo, EDGE)], dst.at[0], dr, 0))
-        near.append(push(src.at[:, pl.ds(lo, EDGE)], dst.at[pl.ds(1, SRC)], dr, 0))
+        near.append(push(ref_h.at[pl.ds(lo, EDGE)], dst.at[0], dr, 0))
+        near.append(push(src_h.at[:, pl.ds(lo, EDGE)], dst.at[pl.ds(1, SRC)], dr, 0))
     for dr, lo, vert in ((-1, 0, 1), (1, last, 0)):
         for dc, cl, side in ((-1, 0, 1), (1, cols - LANES, 0)):
             dst = corner.at[vert, side]
-            near.append(push(ref.at[pl.ds(lo, EDGE), pl.ds(cl, LANES)], dst.at[0], dr, dc))
+            near.append(push(ref_h.at[pl.ds(lo, EDGE), pl.ds(cl, LANES)], dst.at[0], dr, dc))
             near.append(push(
-                src.at[:, pl.ds(lo, EDGE), pl.ds(cl, LANES)], dst.at[pl.ds(1, SRC)], dr, dc
+                src_h.at[:, pl.ds(lo, EDGE), pl.ds(cl, LANES)], dst.at[pl.ds(1, SRC)], dr, dc
             ))
-    for a in range(SRC + 1):
-        image = ref[...] if a == 0 else src[a - 1]
-        xt[a, LEFT : LEFT + cols] = image.T
-    strips = [
-        push(xt.at[:, pl.ds(cols, LEFT)], xt.at[:, pl.ds(0, LEFT)], 0, 1),
-        push(xt.at[:, pl.ds(LEFT, EDGE)], xt.at[:, pl.ds(LEFT + cols, EDGE)], 0, -1),
-    ]
     coarse = []
     for o in range(1, nc):
         for a, b in ((cd_ref, disp), (cc_ref, conf)):
             coarse.append(push(a, b.at[pl.ds(mine, block)], 0, o))
+    strips = []
+    loads[0].wait()
+    loads[1].wait()
+    for a in range(1, SRC + 1):
+        xt[a, LEFT : LEFT + cols] = src[a - 1].T
+        strips.append(push(xt.at[a, pl.ds(cols, LEFT)], xt.at[a, pl.ds(0, LEFT)], 0, 1))
+    xt[0, LEFT : LEFT + cols] = ref[...].T
+    strips.append(push(
+        xt.at[0, pl.ds(LEFT + cols - EDGE, EDGE)], xt.at[0, pl.ds(LEFT - EDGE, EDGE)], 0, 1
+    ))
+    strips.append(push(
+        xt.at[:, pl.ds(LEFT, EDGE)], xt.at[:, pl.ds(LEFT + cols, EDGE)], 0, -1
+    ))
+
+    loads[5].wait()
 
     def hyp_step(k, carry):
         work[...] = hyp[k].astype(F32).T
@@ -149,9 +158,19 @@
         e = kk - LANES - 2 * EDGE * v
         pos = jnp.where(kk < LANES, kk, jnp.where(e < EDGE, e - EDGE, LANES + e - EDGE))
         ok = (jnp.abs(pos - oo) <= RAD) & ((kk < LANES) | ((e >= 0) & (e < 2 * EDGE)))
-        band[v] = jnp.where(ok, 1.0, 0.0).astype(BF16)
-
-    for copy in coarse:
+        for i in range(3):
+            band[v, 2 * LANES * i : 2 * LANES * (i + 1)] = jnp.where(ok, 1.0, 0.0).astype(BF16)
+
+    def own_spread(b, carry):
+        for k in range(8):
+            u = LEFT + b * 8 + k
+            for a in range(SRC + 1):
+                ov[a, u] = xt[a, pl.ds(u, Q, stride=tt), :]
+        return carry
+
+    lax.fori_loop(0, tt // 8, own_spread, 0)
+
+    for copy in coarse + loads[2:5]:
         copy.wait()
     win = ct + 2 * PADC
     start = pl.multiple_of(ct * r, 8)
@@ -207,31 +226,41 @@
         xe[w, 0:LEFT] = x[LANES - LEFT :]
     for w, x in halo_rows(lambda a: corner[0, 1, a], lambda a: corner[1, 1, a], rside):
         xe[w, LEFT + cols : LEFT + cols + EDGE] = x[:EDGE]
+    def spread(b, carry):
+        for k in range(8):
+            u = b * 8 + k
+            for w in range(2):
+                ove[w, u] = xe[w, pl.ds(u, Q, stride=tt), :]
+        return carry
+
+    lax.fori_loop(0, uu // 8, spread, 0)
     for copy in strips:
         copy.wait()
 
     @pl.when(c == 0)
     def _():
-        xt[:, 0:LEFT] = jnp.zeros((SRC + 1, LEFT, LANES), F32)
+        xt[1:, 0:LEFT] = jnp.zeros((SRC, LEFT, LANES), F32)
+        xt[0, LEFT - EDGE : LEFT] = jnp.zeros((EDGE, LANES), F32)
 
     @pl.when(c == nc - 1)
     def _():
         xt[:, LEFT + cols : LEFT + cols + EDGE] = jnp.zeros((SRC + 1, EDGE, LANES), F32)
 
-    def spread(b, carry):
+    def halo_spread(b, carry):
         for k in range(8):
-            u = b * 8 + k
-            for a in range(SRC + 1):
+            u = lax.rem(b * 8 + LEFT + tt, uu) + k
+            for a in range(1, SRC + 1):
                 ov[a, u] = xt[a, pl.ds(u, Q, stride=tt), :]
-            for w in range(2):
-                ove[w, u] = xe[w, pl.ds(u, Q, stride=tt), :]
-        return carry
-
-    lax.fori_loop(0, uu // 8, spread, 0)
+        return carry
+
+    lax.fori_loop(0, (uu - tt) // 8, halo_spread, 0)
+    for k in range(EDGE):
+        for u in (LEFT - EDGE + k, LEFT + tt + k):
+            ov[0, u] = xt[0, pl.ds(u, Q, stride=tt), :]
 
     def mean_and_scale(x, e, n, v):
-        means = row_box(split3(col_box(x, n)), e[0], band[v]) * (1.0 / AREA)
-        squares = row_box(split3(col_box(x * x, n)), e[1], band[v]) * (1.0 / AREA)
+        means = row_box(split3(col_box(x, n)), e[0], band.at[v]) * (1.0 / AREA)
+        squares = row_box(split3(col_box(x * x, n)), e[1], band.at[v]) * (1.0 / AREA)
         return means, lax.rsqrt(squares - means * means + FLOOR)
 
     mb = 16
@@ -243,29 +272,30 @@
         e = ove[0, pl.ds(off + at, mb + WIN - 1)]
         es = split3(col_box(e, mb)), split3(col_box(e * e, mb))
         mean, scale = mean_and_scale(x, es, mb, 0)
-        rmom[0, pl.ds(at, mb)] = mean
+        rmom[0, pl.ds(at, mb)] = mean * AREA
         rmom[1, pl.ds(at, mb)] = scale * (1.0 / SRC)
         return carry
 
     lax.fori_loop(0, tt // mb, ref_moments, 0)
 
+    mb2 = ww // 2
     def src_moments(b, carry):
-        at = b * mb
+        at = b * mb2
         u = at + off - MLEFT
-        e = ove[1, pl.ds(u, mb + WIN - 1)]
-        es = split3(col_box(e, mb)), split3(col_box(e * e, mb))
+        e = ove[1, pl.ds(u, mb2 + WIN - 1)]
+        es = split3(col_box(e, mb2)), split3(col_box(e * e, mb2))
         for v in range(SRC):
-            x = ov[v + 1, pl.ds(u, mb + WIN - 1)]
-            mean, scale = mean_and_scale(x, es, mb, v)
-            mom[v, 0, pl.ds(at, mb)] = mean
-            mom[v, 1, pl.ds(at, mb)] = scale
-        return carry
-
-    lax.fori_loop(0, ww // mb, src_moments, 0)
+            x = ov[v + 1, pl.ds(u, mb2 + WIN - 1)]
+            mean, scale = mean_and_scale(x, es, mb2, v)
+            mom[v, 0, pl.ds(at, mb2)] = mean
+            mom[v, 1, pl.ds(at, mb2)] = scale * (1.0 / AREA)
+        return carry
+
+    lax.fori_loop(0, ww // mb2, src_moments, 0)
 
     sel[...] = jnp.zeros(sel.shape, F32)
     group = lax.shift_right_logical(iota((1, Q, LANES), 2), jnp.full((1, Q, LANES), 4))
-    tb = 16
+    tb = 32
     span = tb + WIN - 1
 
     def level(i, carry):
@@ -281,7 +311,7 @@
         total = None
         for v in range(SRC):
             y = col_box(x0 * ov[v + 1, pl.ds(off + at - moved[v], span)], tb)
-            cross = row_box(split3(y), es, band[v]) * (1.0 / AREA)
+            cross = row_box(split3(y), es, band.at[v])
             wi = MLEFT + at - moved[v]
             part = (cross - mr * mom[v, 0, pl.ds(wi, tb)]) * mom[v, 1, pl.ds(wi, tb)]
             total = part if total is None else total + part
@@ -343,21 +373,25 @@
     gi = r * rows + lane2
     rcount = 4.0 - jnp.where(gi == 0, 1.0, 0.0) - jnp.where(gi == nr * rows - 1, 1.0, 0.0)
 
-    def black_step(t, carry):
-        red = redt[pl.ds(EDGE + t, Q, stride=tt), :]
-        nb = redt[pl.ds(EDGE - 1 + t, Q, stride=tt), :] + redt[pl.ds(EDGE + 1 + t, Q, stride=tt), :]
-        nb = nb + jnp.where(lane2 == 0, 0.0, pltpu.roll(red, 1, 1))
-        nb = nb + jnp.where(lane2 == LANES - 1, 0.0, pltpu.roll(red, LANES - 1, 1))
-        nb = nb + edge[pl.ds(t, Q, stride=tt), :]
-        gj = c * cols + chunk * tt + t
-        count = rcount - jnp.where(gj == 0, 1.0, 0.0) - jnp.where(gj == nc * cols - 1, 1.0, 0.0)
-        centre = 0.5 * ups[t] + 0.5 * nb / count
-        black = estimate(t, 1, centre[None])[0]
-        even = lax.rem(gi + gj, 2) == 0
-        work[pl.ds(t, Q, stride=tt), :] = jnp.where(even, red, black)
-        return carry
-
-    lax.fori_loop(0, tt, black_step, 0)
+    def black_step(b, carry):
+        for t in [b * bb + k for k in range(bb)]:
+            red = redt[pl.ds(EDGE + t, Q, stride=tt), :]
+            nb = redt[pl.ds(EDGE - 1 + t, Q, stride=tt), :]
+            nb = nb + redt[pl.ds(EDGE + 1 + t, Q, stride=tt), :]
+            nb = nb + jnp.where(lane2 == 0, 0.0, pltpu.roll(red, 1, 1))
+            nb = nb + jnp.where(lane2 == LANES - 1, 0.0, pltpu.roll(red, LANES - 1, 1))
+            nb = nb + edge[pl.ds(t, Q, stride=tt), :]
+            gj = c * cols + chunk * tt + t
+            count = rcount - jnp.where(gj == 0, 1.0, 0.0)
+            count = count - jnp.where(gj == nc * cols - 1, 1.0, 0.0)
+            centre = 0.5 * ups[t] + 0.5 * nb / count
+            black = estimate(t, 1, centre[None])[0]
+            even = lax.rem(gi + gj, 2) == 0
+            work[pl.ds(t, Q, stride=tt), :] = jnp.where(even, red, black)
+        return carry
+
+    bb = 4
+    lax.fori_loop(0, tt // bb, black_step, 0)
     out[...] = work[...].T
 
 
@@ -368,15 +402,20 @@
     uu = LEFT + tt + EDGE
     ww = MLEFT + tt
     full = LEFT + cols + EDGE
-    count = 4 + 8 + 2 + 2 * (nc - 1) + 4
+    count = 4 + 8 + 6 + 2 * (nc - 1) + 4
     v = lambda *s: pltpu.VMEM(s, F32)
     vmem = pl.BlockSpec(memory_space=pltpu.VMEM)
     return pl.pallas_call(
         functools.partial(kernel, nr, nc),
         out_shape=jax.ShapeDtypeStruct((rows, cols), F32),
-        in_specs=[pl.BlockSpec(memory_space=pltpu.SMEM)] + [vmem] * 5,
+        in_specs=[pl.BlockSpec(memory_space=pl.ANY)] * 6,
         out_specs=vmem,
         scratch_shapes=[
+            pltpu.SMEM((SRC,), jnp.int32),
+            v(rows, cols),
+            v(SRC, rows, cols),
+            pltpu.VMEM((HYP, rows, cols), jnp.int32),
+            pltpu.SemaphoreType.DMA((6,)),
             v(SRC + 1, full, LANES),
             v(SRC + 1, EDGE, cols),
             v(SRC + 1, EDGE, cols),
@@ -390,7 +429,7 @@
             v(HYP, tt, Q, LANES),
             v(block * nc + 2 * PADC, ncc),
             v(block * nc + 2 * PADC, ncc),
-            pltpu.VMEM((SRC, 2 * LANES, LANES), BF16),
+            pltpu.VMEM((SRC, 6 * LANES, LANES), BF16),
             v(cols + 2 * EDGE, LANES),
             v(4, EDGE, cols),
             v(cols, LANES),
@@ -400,7 +439,7 @@
             pltpu.SemaphoreType.DMA((count,)),
         ],
         compiler_params=pltpu.CompilerParams(
-            collective_id=0, has_side_effects=True, vmem_limit_bytes=48 * 1024 * 1024
+            collective_id=0, has_side_effects=True, vmem_limit_bytes=60 * 1024 * 1024
         ),
         name="stereo",
     )(source_ids, reference_image, source_images, hypotheses, disp, conf)

time: 49.1 us -> 37.8 us (0.77)
  Pallas kernels: 42.8 us -> 36.1 us
  local copies, waits for them, and re-layouts: 5.92 us -> 1.57 us
    pallas_call x1, Pallas kernels: 42.8 us -> 36.1 us  [on_device(): pl.pallas_call(functools.partial(kernel, nr, nc), out_shape=jax.ShapeDtyp...]
    unnamed x13 -> x1, local copies, waits for them, and re-layouts: 5.92 us -> 1.57 us
where the time goes in v2:
time: 37.8 us; the launch traced here: 37.7 us
  Pallas kernels  36.1 us (96%)
  local copies, waits for them, and re-layouts  1.57 us (4%)
    pallas_call x1, Pallas kernels, on_device(): pl.pallas_call(functools.partial(kernel, nr, nc), out_shape=jax.ShapeDtyp...  36.1 us
    unnamed x1, local copies, waits for them, and re-layouts  1.57 us

profile of v2, /device:TPU:0, one launch (start us, length us, event | category | flops | bytes accessed | tf_op | source)
XLA Modules:
  0.0 37.7 jit_solution(10445431983715899740)
XLA Ops:
  0.0 36.1 %stereo.1 = f32[128,256]{1,0:T(8,128)} custom-call(s32[4]{0:T(128)} %ids_h.1, f32[128,256]{1,0:T(8,128)} %ref_h.1, f32[4,128,256]{2,1,0:T(8,128)} %src_h.1, s32[8,128,256]{2,1,0:T(8,128)} %hyp_h.1, f32[32,128]{1,0:T(8,128)} %cd_ref.1, f32[32,128]{1,0:T(8,128)} %cc_ref.1), custom_call_target="tpu_custom_call" | custom-call | tf_op jit(solution)/shard_map/stereo/pallas_call | solution.py:408
  36.1 1.6 %copy.8 = f32[128,256]{1,0:T(8,128)} copy(f32[128,256]{1,0:T(8,128)} %stereo.1) | data formatting | bytes 262144
